TPU v7x, 32 devices: a whole 2x2x4 slice. The times are simulated.
32 devices in a mesh: kgrp: 8 (over y, x, core), img: 4 (over z).
Axes of the slice: x: 2, y: 2, z: 4, core: 2. Of those that a mesh axis runs over, the one named last changes fastest.
Arguments:
- vectors: float32 [2, 16, 1024], P(None, 'img', 'kgrp'), may hold values from -6 to 6
- conduction: bfloat16 [16, 2, 8, 4, 4096], P('kgrp', None, None, 'img'), may hold values from -6 to 6
- valence: bfloat16 [16, 2, 8, 4, 4096], P('kgrp', None, None, 'img'), may hold values from -6 to 6
- hole_point: int32 [1], replicated, may hold values from 0 to 16383
- kpoint_grid: int32 [3, 16], replicated, may hold values from 0 to 11
- image_cells: int32 [3, 512], replicated, may hold values from -6 to 6
Outputs:
- psi_real: float32 [16, 4, 4096, 512], P(None, 'img', 'kgrp')
- psi_imag: float32 [16, 4, 4096, 512], P(None, 'img', 'kgrp')
All inputs are finite; a program needn't handle non-finite values.
Results may differ from a plain program's by a relative error of at most 0.0043.
Values may be sent and summed in bfloat16 or wider, within the bound.
No kernel may reach another device: no remote copies, remote signals or barrier semaphores. Data moves between devices by JAX's collectives and lax.ppermute only.
A program may use at most 128 MiB of HBM per device.

v0:
```python
import jax
import jax.numpy as jnp
import numpy as np
from jax import lax
from jax.sharding import PartitionSpec as P

NV = 8
NC = 8
cosine_levels = np.cos(2.0 * np.pi * np.arange(12) / 12.0)
sine_levels = np.sin(2.0 * np.pi * np.arange(12) / 12.0)


def phase_table(kpoint_grid, image_cells):
    turn_count = kpoint_grid[0][:, None] * image_cells[0][None, :]
    turn_count = turn_count + kpoint_grid[1][:, None] * image_cells[1][None, :]
    turn_count = turn_count + kpoint_grid[2][:, None] * image_cells[2][None, :]
    turn_count = jnp.mod(turn_count, 12)
    cosine = jnp.zeros(turn_count.shape, jnp.float32)
    sine_part = jnp.zeros(turn_count.shape, jnp.float32)
    for level_index in range(12):
        matches = turn_count == level_index
        cosine = jnp.where(matches, jnp.float32(cosine_levels[level_index]), cosine)
        sine_part = jnp.where(matches, jnp.float32(sine_levels[level_index]), sine_part)
    upper_half = jnp.stack([cosine, sine_part], 1)
    lower_half = jnp.stack([-sine_part, cosine], 1)
    return jnp.stack([upper_half, lower_half], 0).astype(jnp.bfloat16)


def hole_weights(amplitudes, hole_values):
    norm_factor = (NV * NC) ** (-0.5)
    real_amplitude = amplitudes[0]
    imaginary_amplitude = amplitudes[1]
    real_hole = hole_values[:, 0]
    imaginary_hole = hole_values[:, 1]
    highest = lax.Precision.HIGHEST
    weight_real = jnp.einsum("skvc,kv->ksc", real_amplitude, real_hole, precision=highest)
    weight_real = weight_real + jnp.einsum(
        "skvc,kv->ksc", imaginary_amplitude, imaginary_hole, precision=highest
    )
    weight_imaginary = jnp.einsum("skvc,kv->ksc", imaginary_amplitude, real_hole, precision=highest)
    weight_imaginary = weight_imaginary - jnp.einsum(
        "skvc,kv->ksc", real_amplitude, imaginary_hole, precision=highest
    )
    return jnp.stack([weight_real * norm_factor, weight_imaginary * norm_factor], 1).astype(
        jnp.bfloat16
    )


def mixing(weights):
    weight_real = weights[:, 0]
    weight_imaginary = weights[:, 1]
    first_row = jnp.stack([weight_real, -weight_imaginary], 2)
    second_row = jnp.stack([weight_imaginary, weight_real], 2)
    return jnp.stack([first_row, second_row], 1)


def shards(vectors, conduction, valence, hole_point, kpoint_grid, image_cells):
    group_size = lax.axis_size("kgrp")
    local_k = conduction.shape[0]
    slab_width = conduction.shape[4]
    own_excitons = vectors.shape[1]
    blocks = vectors.shape[2] // group_size
    columns = vectors.reshape(2, own_excitons, group_size, blocks)
    owned_columns = lax.all_to_all(columns, "kgrp", split_axis=2, concat_axis=2, tiled=True)
    owned_columns = owned_columns.reshape(2, own_excitons, local_k, NV, NC)
    hole_offset = hole_point[0] % slab_width
    hole_slab = hole_point[0] // slab_width
    present = (lax.axis_index("img") == hole_slab).astype(jnp.float32)
    picked = (
        lax.dynamic_slice_in_dim(valence[:, :, :, 0, :], hole_offset, 1, 3)[..., 0].astype(
            jnp.float32
        )
        * present
    )
    hole_values = lax.psum(picked, "img")
    weights = lax.all_gather(hole_weights(owned_columns, hole_values), "img", axis=2, tiled=True)
    phases = phase_table(kpoint_grid, image_cells)
    products = jnp.einsum(
        "kasbc,kbcp->sakp",
        mixing(weights),
        conduction[:, :, :, 0, :],
        preferred_element_type=jnp.float32,
    ).astype(jnp.bfloat16)
    summed = jnp.einsum(
        "sakp,akbn->spbn",
        lax.all_to_all(products, "kgrp", split_axis=3, concat_axis=2, tiled=True),
        phases,
        preferred_element_type=jnp.float32,
    )
    normal_scale = (2 * kpoint_grid.shape[1]) ** (-0.5)
    summed = summed * normal_scale
    return (summed[:, None, :, 0, :], summed[:, None, :, 1, :])


def solution(mesh):
    placed = (
        P(None, "img", "kgrp"),
        P("kgrp", None, None, "img", None),
        P("kgrp", None, None, "img", None),
        P(),
        P(),
        P(),
    )
    return jax.shard_map(
        shards,
        mesh=mesh,
        in_specs=placed,
        out_specs=(P(None, "img", "kgrp", None), P(None, "img", "kgrp", None)),
        check_vma=False,
    )
```

profile of v0, /device:TPU:0, one launch (start us, length us, event | category | flops | bytes accessed | tf_op | source)
XLA Modules:
  0.0 113.5 jit_solution(17862852057084318996)
XLA Ops:
  0.6 0.0 copy-start
  0.6 0.8 reshape.639
  1.5 0.7 reshape.653
  2.2 5.2 %all-to-all-start = ((f32[8,1,128]{2,1,0:T(1,128)}), f32[8,1,128]{2,1,0:T(1,128)S(1)}, u32[]{:S(2)}, u32[]{:S(2)}) async-start(f32[8,1,128]{2,1,0:T(1,128)} %reshape.653), calls=%async_computation | async-start | bytes 8192 | tf_op jit(solution)/shard_map/all_to_all | solution.py:64
  7.4 0.8 fusion.27
  8.9 0.9 multiply_reduce_fusion
  9.7 11.9 %psum.7 = f32[2,2,8]{2,1,0:T(2,128)S(1)} all-reduce(f32[2,2,8]{2,1,0:T(2,128)S(1)} %multiply_reduce_fusion), channel_id=1, replica_groups=mesh['kgrp'=8,'img'=4] {'img'}, use_global_device_ids=true, to_apply=%region_0.1 | all-reduce | flops 32 | bytes 256 | tf_op jit(solution)/shard_map/psum | solution.py:75
  21.7 0.0 all-to-all-done
  21.7 0.5 broadcast.739
  22.2 0.7 reduce.2
  22.8 0.1 reshape.654
  23.0 0.1 squeeze.26
  23.0 0.2 fusion.13
  23.2 0.2 fusion.15
  23.4 0.1 squeeze.28
  23.4 0.2 fusion.9
  23.6 0.2 fusion.11
  23.8 13.2 %all_gather.3 = bf16[2,2,16,8]{3,1,0,2:T(2,128)(2,1)S(1)} all-gather(bf16[2,2,4,8]{3,1,0,2:T(2,128)(2,1)S(1)} %copy.34), channel_id=1, replica_groups=mesh['kgrp'=8,'img'=4] {'img'}, dimensions={2}, use_global_device_ids=true | all-gather | bytes 1280 | tf_op jit(solution)/shard_map/all_gather | solution.py:76
  37.1 0.1 copy.56
  37.2 0.1 copy.55
  37.3 0.0 copy-done
  37.3 0.3 fusion.1
  37.6 6.9 %copy.38 = bf16[16,2,2,4096]{0,1,2,3:T(2,128)(2,1)} copy(bf16[16,2,2,4096]{3,0,1,2:T(8,128)(2,1)S(1)} %fusion.1) | data formatting | bytes 1048576 | tf_op jit(solution)/shard_map/convert_element_type | solution.py:83
  44.5 6.5 %reshape.655 = bf16[8,2,16384]{2,1,0:T(2,128)(2,1)} reshape(bf16[4096,2,2,16]{3,2,1,0:T(2,128)(2,1)} %bitcast.101) | data formatting | bytes 1048576
  51.0 4.2 %all-to-all-start.1 = ((bf16[8,2,16384]{2,1,0:T(2,128)(2,1)}), bf16[8,2,16384]{2,1,0:T(2,128)(2,1)S(1)}, u32[]{:S(2)}, u32[]{:S(2)}) async-start(bf16[8,2,16384]{2,1,0:T(2,128)(2,1)} %reshape.655), calls=%async_computation.1 | async-start | bytes 1048576 | tf_op jit(solution)/shard_map/all_to_all | solution.py:86
  55.2 0.8 slice_bitcast_fusion.6
  56.0 0.1 fusion.20
  56.1 8.8 %all-to-all-done.1 = bf16[8,2,16384]{2,1,0:T(2,128)(2,1)S(1)} async-done(((bf16[8,2,16384]{2,1,0:T(2,128)(2,1)}), bf16[8,2,16384]{2,1,0:T(2,128)(2,1)S(1)}, u32[]{:S(2)}, u32[]{:S(2)}) %all-to-all-start.1) | async-done | bytes 524320 | tf_op jit(solution)/shard_map/all_to_all | solution.py:86
  64.9 4.1 %reshape.656 = bf16[4096,2,2,16]{3,2,1,0:T(2,128)(2,1)} reshape(bf16[8,2,16384]{2,1,0:T(2,128)(2,1)S(1)} %all-to-all-done.1) | data formatting | bytes 1048576
  68.9 9.7 %copy.39 = bf16[16,2,2,8,512]{4,2,3,1,0:T(2,128)(2,1)S(1)} copy(bf16[16,2,2,8,512]{0,1,2,4,3:T(2,128)(2,1)} %bitcast.102) | data formatting | bytes 1048576 | tf_op jit(solution)/shard_map/all_to_all | solution.py:86
  78.7 0.2 reshape.648
  78.9 13.1 %bitcast_multiply_fusion = f32[16,512,2,512]{3,1,2,0:T(8,128)} fusion(bf16[16,2,16,512,1]{3,2,1,0,4:T(8,128)(2,1)S(1)} %reshape.648, bf16[1,16,2,512]{3,1,0,2:T(8,128)(2,1)S(1)} %get-tuple-element.15, bf16[1,16,2,512]{3,1,0,2:T(8,128)(2,1)S(1)} %get-tuple-element.14), kind=kOutput, calls=%fused_computation | convolution fusion | flops 545390592 | bytes 34144256 | tf_op jit(solution)/shard_map/sakp,akbn->spbn/dot_general | solution.py:84
  91.9 0.0 copy-start.1
  91.9 21.5 %slice_bitcast_fusion = (f32[16,1,512,512]{3,2,1,0:T(8,128)}, f32[16,1,512,512]{3,2,1,0:T(8,128)}) fusion(f32[16,512,2,512]{3,1,2,0:T(8,128)} %bitcast_multiply_fusion), kind=kLoop, calls=%fused_computation.1 | loop fusion | bytes 67108864
  113.5 0.0 copy-done.1
  (11 shorter events, 0.1 us)
Async XLA Ops:
  0.6 36.6 %copy-start = (bf16[2,2,8,1,4096]{4,2,3,1,0:T(8,128)(2,1)S(1)}, bf16[2,2,8,1,4096]{4,2,3,1,0:T(8,128)(2,1)}, u32[]{:S(2)}) copy-start(bf16[2,2,8,1,4096]{4,2,3,1,0:T(8,128)(2,1)} %param.7) | copy-start | bytes 786436
  2.2 19.5 %all-to-all-start = ((f32[8,1,128]{2,1,0:T(1,128)}), f32[8,1,128]{2,1,0:T(1,128)S(1)}, u32[]{:S(2)}, u32[]{:S(2)}) async-start(f32[8,1,128]{2,1,0:T(1,128)} %reshape.653), calls=%async_computation | async-start | bytes 8192 | tf_op jit(solution)/shard_map/all_to_all | solution.py:64
  51.0 13.9 %all-to-all-start.1 = ((bf16[8,2,16384]{2,1,0:T(2,128)(2,1)}), bf16[8,2,16384]{2,1,0:T(2,128)(2,1)S(1)}, u32[]{:S(2)}, u32[]{:S(2)}) async-start(bf16[8,2,16384]{2,1,0:T(2,128)(2,1)} %reshape.655), calls=%async_computation.1 | async-start | bytes 1048576 | tf_op jit(solution)/shard_map/all_to_all | solution.py:86
  91.9 21.5 %copy-start.1 = (bf16[2,2,8,1,4096]{4,2,3,1,0:T(8,128)(2,1)S(1)}, bf16[2,2,8,1,4096]{4,2,3,1,0:T(8,128)(2,1)}, u32[]{:S(2)}) copy-start(bf16[2,2,8,1,4096]{4,2,3,1,0:T(8,128)(2,1)} %param.7) | copy-start | bytes 786436
where the time goes:
time: 114 us; the launch traced here: 113 us
  local copies, waits for them, and re-layouts  53 us (46%)
  blocking collectives  25.2 us (22%)
  matrix products  14.1 us (12%)
  starting transfers between devices  9.4 us (8%)
  waiting for transfers between devices  8.76 us (8%)
  other arithmetic  1.71 us (2%)
  between operations  1.44 us (1%)
    unnamed x11, local copies, waits for them, and re-layouts  33 us
    all_gather x1, blocking collectives, shards(): lax.all_gather(hole_weights(owned_columns, hole_values), 'img', axis=2, t...  13.2 us
    dot_general x1, matrix products, shards(): jnp.einsum('sakp,akbn->spbn', lax.all_to_all(products, 'kgrp', split_axis...  13.1 us
    psum x1, blocking collectives, shards(): hole_values = lax.psum(picked, 'img')  11.9 us
    all_to_all x2, local copies, waits for them, and re-layouts, shards(): lax.all_to_all(products, 'kgrp', split_axis=3, concat_axis=2, tiled=True)  9.93 us
    all_to_all x1, waiting for transfers between devices, shards(): lax.all_to_all(products, 'kgrp', split_axis=3, concat_axis=2, tiled=True)  8.76 us
    convert_element_type x1, local copies, waits for them, and re-layouts, shards(): products = jnp.einsum('kasbc,kbcp->sakp', mixing(weights), conduction[:,...  6.9 us
    all_to_all x1, starting transfers between devices, shards(): lax.all_to_all(columns, 'kgrp', split_axis=2, concat_axis=2, tiled=True)  5.2 us
  transfers between devices with their start and end apart: 2, of which 1 were waited for; matrix products, arithmetic and copies ran while one was open for 2% of the time, Pallas kernels for 0%

commit v1 on v0

--- a/solution.py
+++ b/solution.py
@@ -83,7 +83,12 @@
     ).astype(jnp.bfloat16)
     summed = jnp.einsum(
         "sakp,akbn->spbn",
-        lax.all_to_all(products, "kgrp", split_axis=3, concat_axis=2, tiled=True),
+        jnp.concatenate(
+            lax.all_to_all(
+                jnp.stack(jnp.split(products, lax.axis_size("kgrp"), axis=3)), "kgrp", 0, 0
+            ),
+            axis=2,
+        ),
         phases,
         preferred_element_type=jnp.float32,
     )

time: 114 us -> 91.6 us (0.80)
  local copies, waits for them, and re-layouts: 53 us -> 30.7 us
    all_to_all x2 -> x0, local copies, waits for them, and re-layouts: 9.93 us -> none  [shards(): lax.all_to_all(products, 'kgrp', split_axis=3, concat_axis=2, tiled=True)]
    convert_element_type x1 -> x0, local copies, waits for them, and re-layouts: 6.9 us -> none  [shards(): products = jnp.einsum('kasbc,kbcp->sakp', mixing(weights), conduction[:,...]
    unnamed x11 -> x16, local copies, waits for them, and re-layouts: 33 us -> 26.9 us
  transfers between devices with their start and end apart: 2 -> 2, of which waited for: 1 -> 1; matrix products, arithmetic and copies ran while one was open for 2% -> 3% of each run, Pallas kernels for 0% -> 0%
where the time goes in v1:
time: 91.6 us; the launch traced here: 91.2 us
  local copies, waits for them, and re-layouts  30.7 us (34%)
  blocking collectives  25.2 us (28%)
  matrix products  14.1 us (15%)
  starting transfers between devices  9.4 us (10%)
  waiting for transfers between devices  8.76 us (10%)
  other arithmetic  1.71 us (2%)
  between operations  1.43 us (2%)
    unnamed x16, local copies, waits for them, and re-layouts  26.9 us
    all_gather x1, blocking collectives, shards(): lax.all_gather(hole_weights(owned_columns, hole_values), 'img', axis=2, t...  13.2 us
    dot_general x1, matrix products, shards(): jnp.einsum('sakp,akbn->spbn', jnp.concatenate(lax.all_to_all(jnp.stack(jn...  13.1 us
    psum x1, blocking collectives, shards(): hole_values = lax.psum(picked, 'img')  11.9 us
    all_to_all x1, waiting for transfers between devices, shards(): lax.all_to_all(jnp.stack(jnp.split(products, lax.axis_size('kgrp'), axis=...  8.76 us
    all_to_all x1, starting transfers between devices, shards(): lax.all_to_all(columns, 'kgrp', split_axis=2, concat_axis=2, tiled=True)  5.2 us
    all_to_all x1, starting transfers between devices, shards(): lax.all_to_all(jnp.stack(jnp.split(products, lax.axis_size('kgrp'), axis=...  4.2 us
  transfers between devices with their start and end apart: 2, of which 1 were waited for; matrix products, arithmetic and copies ran while one was open for 3% of the time, Pallas kernels for 0%

profile of v1, /device:TPU:0, one launch (start us, length us, event | category | flops | bytes accessed | tf_op | source)
XLA Modules:
  0.0 91.2 jit_solution(5312893566767054547)
XLA Ops:
  0.6 0.0 copy-start
  0.6 0.8 reshape.645
  1.5 0.7 reshape.660
  2.2 5.2 %all-to-all-start = ((f32[8,1,128]{2,1,0:T(1,128)}), f32[8,1,128]{2,1,0:T(1,128)S(1)}, u32[]{:S(2)}, u32[]{:S(2)}) async-start(f32[8,1,128]{2,1,0:T(1,128)} %reshape.660), calls=%async_computation | async-start | bytes 8192 | tf_op jit(solution)/shard_map/all_to_all | solution.py:64
  7.4 0.8 fusion.35
  8.9 0.9 multiply_reduce_fusion
  9.7 11.9 %psum.7 = f32[2,2,8]{2,1,0:T(2,128)S(1)} all-reduce(f32[2,2,8]{2,1,0:T(2,128)S(1)} %multiply_reduce_fusion), channel_id=1, replica_groups=mesh['kgrp'=8,'img'=4] {'img'}, use_global_device_ids=true, to_apply=%region_0.1 | all-reduce | flops 32 | bytes 256 | tf_op jit(solution)/shard_map/psum | solution.py:75
  21.7 0.0 all-to-all-done
  21.7 0.5 broadcast.739
  22.2 0.7 reduce.2
  22.8 0.1 reshape.661
  23.0 0.1 squeeze.26
  23.0 0.2 fusion.21
  23.2 0.2 fusion.23
  23.4 0.1 squeeze.28
  23.4 0.2 fusion.17
  23.6 0.2 fusion.19
  23.8 13.2 %all_gather.3 = bf16[2,2,16,8]{3,1,0,2:T(2,128)(2,1)S(1)} all-gather(bf16[2,2,4,8]{3,1,0,2:T(2,128)(2,1)S(1)} %copy.33), channel_id=1, replica_groups=mesh['kgrp'=8,'img'=4] {'img'}, dimensions={2}, use_global_device_ids=true | all-gather | bytes 1280 | tf_op jit(solution)/shard_map/all_gather | solution.py:76
  37.1 0.1 copy.56
  37.2 0.1 copy.55
  37.3 0.0 copy-done
  37.3 0.3 fusion.1
  37.6 0.6 fusion.11
  38.2 0.6 fusion.10
  38.9 0.6 fusion.9
  39.5 0.6 fusion.8
  40.1 0.6 fusion.7
  40.8 0.6 fusion.6
  41.4 0.6 fusion.5
  42.0 0.6 fusion.4
  42.7 4.2 %all-to-all-start.1 = ((bf16[8,16,2,2,512]{4,1,2,3,0:T(8,128)(2,1)}), bf16[8,16,2,2,512]{4,1,2,3,0:T(8,128)(2,1)S(1)}, u32[]{:S(2)}, u32[]{:S(2)}) async-start(bf16[8,16,2,2,512]{4,1,2,3,0:T(8,128)(2,1)} %fusion.4), calls=%async_computation.1 | async-start | bytes 1048576 | tf_op jit(solution)/shard_map/all_to_all | solution.py:87
  46.9 0.8 slice_bitcast_fusion.14
  47.7 0.1 fusion.28
  47.8 8.8 %all-to-all-done.1 = bf16[8,16,2,2,512]{4,1,2,3,0:T(8,128)(2,1)S(1)} async-done(((bf16[8,16,2,2,512]{4,1,2,3,0:T(8,128)(2,1)}), bf16[8,16,2,2,512]{4,1,2,3,0:T(8,128)(2,1)S(1)}, u32[]{:S(2)}, u32[]{:S(2)}) %all-to-all-start.1) | async-done | bytes 524320 | tf_op jit(solution)/shard_map/all_to_all | solution.py:87
  56.6 0.0 copy-start.1
  56.6 13.1 %bitcast_multiply_fusion = f32[16,512,2,512]{3,1,2,0:T(8,128)} fusion(bf16[16,2,16,512,1]{3,0,1,2,4:T(8,128)(2,1)S(1)} %bitcast.131, bf16[1,16,2,512]{3,1,0,2:T(8,128)(2,1)S(1)} %get-tuple-element.15, bf16[1,16,2,512]{3,1,0,2:T(8,128)(2,1)S(1)} %get-tuple-element.14), kind=kOutput, calls=%fused_computation | convolution fusion | flops 545390592 | bytes 34144256 | tf_op jit(solution)/shard_map/sakp,akbn->spbn/dot_general | solution.py:84
  69.7 21.5 %slice_bitcast_fusion = (f32[16,1,512,512]{3,2,1,0:T(8,128)}, f32[16,1,512,512]{3,2,1,0:T(8,128)}) fusion(f32[16,512,2,512]{3,1,2,0:T(8,128)} %bitcast_multiply_fusion), kind=kLoop, calls=%fused_computation.1 | loop fusion | bytes 67108864
  91.2 0.0 copy-done.1
  (11 shorter events, 0.1 us)
Async XLA Ops:
  0.6 36.6 %copy-start = (bf16[2,2,8,1,4096]{4,2,3,1,0:T(8,128)(2,1)S(1)}, bf16[2,2,8,1,4096]{4,2,3,1,0:T(8,128)(2,1)}, u32[]{:S(2)}) copy-start(bf16[2,2,8,1,4096]{4,2,3,1,0:T(8,128)(2,1)} %param.7) | copy-start | bytes 786436
  2.2 19.5 %all-to-all-start = ((f32[8,1,128]{2,1,0:T(1,128)}), f32[8,1,128]{2,1,0:T(1,128)S(1)}, u32[]{:S(2)}, u32[]{:S(2)}) async-start(f32[8,1,128]{2,1,0:T(1,128)} %reshape.660), calls=%async_computation | async-start | bytes 8192 | tf_op jit(solution)/shard_map/all_to_all | solution.py:64
  42.7 13.9 %all-to-all-start.1 = ((bf16[8,16,2,2,512]{4,1,2,3,0:T(8,128)(2,1)}), bf16[8,16,2,2,512]{4,1,2,3,0:T(8,128)(2,1)S(1)}, u32[]{:S(2)}, u32[]{:S(2)}) async-start(bf16[8,16,2,2,512]{4,1,2,3,0:T(8,128)(2,1)} %fusion.4), calls=%async_computation.1 | async-start | bytes 1048576 | tf_op jit(solution)/shard_map/all_to_all | solution.py:87
  56.6 34.6 %copy-start.1 = (bf16[2,2,8,1,4096]{4,2,3,1,0:T(8,128)(2,1)S(1)}, bf16[2,2,8,1,4096]{4,2,3,1,0:T(8,128)(2,1)}, u32[]{:S(2)}) copy-start(bf16[2,2,8,1,4096]{4,2,3,1,0:T(8,128)(2,1)} %param.7) | copy-start | bytes 786436
